TPU v7x, 32 devices: a whole 2x2x4 slice. The times are simulated.
32 devices in a mesh: lat: 4 (over y, x), lon: 8 (over z, core).
Axes of the slice: x: 2, y: 2, z: 4, core: 2. Of those that a mesh axis runs over, the one named last changes fastest.
Arguments:
- right_side: float32 [512, 1024], P('lat', 'lon'), may hold values from -8 to 8
- surface_term: float32 [512, 1024], P('lat', 'lon'), may hold values from 0.0002 to 0.002
- east_coupling: float32 [512, 1024], P('lat', 'lon'), may hold values from 0.3 to 3
- north_coupling: float32 [512, 1024], P('lat', 'lon'), may hold values from 0.3 to 3
- neast_coupling: float32 [512, 1024], P('lat', 'lon'), may hold values from 0.1 to 0.5
- nwest_coupling: float32 [512, 1024], P('lat', 'lon'), may hold values from 0.1 to 0.5
- land_sea: int32 [512, 1024], P('lat', 'lon'), may hold values from 0 to 1, as said below
- fold_map: int32 [1024], P('lon'), may hold values from 0 to 1023, as said below
Outputs:
- solution: float32 [512, 1024], P('lat', 'lon')
- residual: float32 [512, 1024], P('lat', 'lon')
Inputs may be any that keep to these rules, and one draw needn't show every extreme that they name: fold_map[j] = (c - j) mod 1024 for one odd c: an involution of the columns with no fixed point. land_sea is 0 or 1; land lies in bands of 8 columns, each over one range of rows.
All inputs are finite; a program needn't handle non-finite values.
Results may differ from a plain program's by a relative error of at most 0.0015.
Values sent between devices are 32-bit elements.
A program may use at most 64 MiB of HBM per device.

v0:
```python
import functools

import jax
import jax.numpy as jnp
from jax import lax
from jax.experimental import pallas as pl
from jax.experimental.pallas import tpu as pltpu
from jax.sharding import PartitionSpec as P

ITERS = 8
SUB = 8


def iota(shape, dim):
    return lax.broadcasted_iota(jnp.int32, shape, dim)


def east(x):
    return pltpu.roll(x, x.shape[-1] - 1, x.ndim - 1)


def west(x):
    return pltpu.roll(x, 1, x.ndim - 1)


def from_above(x):
    return pltpu.roll(x, SUB - 1, 0)


def from_below(x):
    return pltpu.roll(x, 1, 0)


def kernel(
    lat_count,
    lon_count,
    shift_ref,
    right_ref,
    surface_ref,
    east_ref,
    north_ref,
    neast_ref,
    nwest_ref,
    land_ref,
    sol_out,
    res_out,
    w_e,
    w_w,
    w_n,
    w_s,
    w_ne,
    w_sw,
    w_nw,
    w_se,
    diag,
    f_a,
    f_g,
    resp0,
    resp1,
    u_ref,
    img,
    dirn,
    along,
    sol_ref,
    res_ref,
    fields,
    msg,
    recv,
    fold_ref,
    top_msg,
    top_recv,
    halo_msg,
    halo_recv,
    pack_msg,
    pack_recv,
    back_msg,
    back_recv,
    send_sem,
    recv_sem,
    top_send,
    top_arrive,
    halo_send,
    halo_arrive,
    pack_send,
    pack_arrive,
    back_send,
    back_arrive,
):
    n_dev = lat_count * lon_count
    lat = lax.axis_index("lat")
    lon = lax.axis_index("lon")
    me = lat * lon_count + lon
    depth, _, width = sol_ref.shape
    own = width // lat_count
    half = depth // 2
    top = depth - 1

    barrier = pltpu.get_barrier_semaphore()

    def greet(step, carry):
        peer = lax.rem(me + step, n_dev)
        pl.semaphore_signal(
            barrier,
            inc=1,
            device_id=(peer // lon_count, lax.rem(peer, lon_count)),
            device_id_type=pl.DeviceIdType.MESH,
        )
        return carry

    lax.fori_loop(1, n_dev, greet, 0, unroll=n_dev <= 64)

    lane = iota((1, width), 1)
    relative = lax.rem(lane - lat * own + width, width)
    own_row = relative < own

    def copy_to(parity, step):
        peer = lax.rem(me + step, n_dev)
        return pltpu.make_async_remote_copy(
            src_ref=msg.at[parity],
            dst_ref=recv.at[parity, me],
            send_sem=send_sem.at[parity, step],
            recv_sem=recv_sem.at[parity, step],
            device_id=(peer // lon_count, lax.rem(peer, lon_count)),
            device_id_type=pl.DeviceIdType.MESH,
        )

    def send_all(parity, row):
        msg[parity] = row
        recv[parity, me] = row

        def one(step, carry):
            copy_to(parity, step).start()
            return carry

        lax.fori_loop(1, n_dev, one, 0, unroll=n_dev <= 64)

    def wait_all(parity):
        def one(step, carry):
            copy_to(parity, step).wait()
            return carry

        lax.fori_loop(1, n_dev, one, 0, unroll=n_dev <= 64)
        top_row = jnp.zeros((lon_count, width), jnp.float32)
        rest = jnp.zeros((lon_count, width), jnp.float32)
        for place in range(lat_count):
            rows = jnp.concatenate(
                [recv[parity, place * lon_count + b] for b in range(lon_count)], axis=0
            )
            offset = lax.rem(iota((lon_count, width), 1) - place * own + width, width)
            top_row = top_row + jnp.where(offset < own, rows, 0.0)
            moved = pltpu.roll(rows, width - own, 1)
            rest = rest + jnp.where(offset < own, moved, 0.0)
        return top_row, rest

    mesh_id = pl.DeviceIdType.MESH
    rows = right_ref.shape[0]
    halo = ITERS
    span = own + 2 * halo
    pl.semaphore_wait(barrier, n_dev - 1)

    at_top = lat == lat_count - 1
    top_msg[0:1] = north_ref[rows - 1 :, :]
    top_msg[1:2] = land_ref[rows - 1 :, :].astype(jnp.float32)

    def top_copy(step):
        peer = lax.rem(me + step, n_dev)
        return pltpu.make_async_remote_copy(
            src_ref=top_msg,
            dst_ref=top_recv.at[lon],
            send_sem=top_send.at[step],
            recv_sem=top_arrive.at[lon],
            device_id=(peer // lon_count, lax.rem(peer, lon_count)),
            device_id_type=mesh_id,
        )

    @pl.when(at_top)
    def _():
        top_recv[lon] = top_msg[...]

        def one(step, carry):
            top_copy(step).start()
            return carry

        lax.fori_loop(1, n_dev, one, 0, unroll=n_dev <= 64)

    given = (right_ref, surface_ref, east_ref, north_ref, neast_ref, nwest_ref, land_ref)
    count = len(given)

    def local(index, v):
        return given[index][v * SUB : (v + 1) * SUB, :].astype(jnp.float32)

    wide = iota((SUB, width), 1)

    def halo_copy(side):
        step = lon_count - 1 if side else 1
        return pltpu.make_async_remote_copy(
            src_ref=halo_msg.at[side],
            dst_ref=halo_recv.at[side],
            send_sem=halo_send.at[side],
            recv_sem=halo_arrive.at[side],
            device_id=(lat, lax.rem(lon + step, lon_count)),
            device_id_type=mesh_id,
        )

    for v in range(rows // SUB):
        eastward = jnp.zeros((SUB, width), jnp.float32)
        westward = eastward
        for i in range(count):
            turned = pltpu.roll(local(i, v), halo * (i + 1), 1)
            slot = wide // halo
            eastward = jnp.where(slot == i, turned, eastward)
            westward = jnp.where(slot == i + 1, turned, westward)
        halo_msg[0, v * SUB : (v + 1) * SUB] = eastward
        halo_msg[1, v * SUB : (v + 1) * SUB] = westward
    halo_copy(0).start()
    halo_copy(1).start()

    def pack(place):
        for v in range(rows // SUB):
            sl = slice(v * SUB, (v + 1) * SUB)
            values = [local(i, v) for i in range(count)]

            def window(i, shift):
                out = pltpu.roll(values[i], (shift - (place * own - halo)) % width, 1)
                if place == 0:
                    left = pltpu.roll(halo_recv[0, sl], (shift - halo * i) % width, 1)
                    out = jnp.where((wide >= shift) & (wide < shift + halo), left, out)
                if place == lat_count - 1:
                    low = shift + halo + own
                    right = pltpu.roll(halo_recv[1, sl], (low - halo * (i + 1)) % width, 1)
                    out = jnp.where((wide >= low) & (wide < low + halo), right, out)
                return out

            first, second = wide < span, wide < 2 * span
            third = wide < 2 * span + halo
            pack_msg[place, 0, sl] = jnp.where(
                first, window(0, 0), jnp.where(second, window(1, span), window(6, 2 * span - halo))
            )
            edge = jnp.where(third, window(6, 2 * span), window(6, 2 * span - own))
            pack_msg[place, 1, sl] = jnp.where(
                first, window(2, 0), jnp.where(second, window(3, span), edge)
            )
            pack_msg[place, 2, sl] = jnp.where(first, window(4, 0), window(5, span))

    here = pl.ds(pl.multiple_of(lat * rows, rows), rows)

    def pack_copy(place):
        return pltpu.make_async_remote_copy(
            src_ref=pack_msg.at[place],
            dst_ref=pack_recv.at[:, here],
            send_sem=pack_send.at[place],
            recv_sem=pack_arrive.at[lat],
            device_id=(place, lon),
            device_id_type=mesh_id,
        )

    for place in [*range(1, lat_count - 1), 0, lat_count - 1]:
        if place == 0:
            halo_copy(0).wait()
            halo_copy(1).wait()
        pack(place)

        @pl.when(lat != place)
        def _(place=place):
            pack_copy(place).start()

    pack_recv[:, here] = pack_msg[lat]
    for place in range(lat_count):

        @pl.when(lat != place)
        def _(place=place):
            pack_copy(place).wait_send()
            pltpu.make_async_remote_copy(
                src_ref=pack_msg.at[place],
                dst_ref=pack_recv.at[:, place * rows : (place + 1) * rows],
                send_sem=pack_send.at[place],
                recv_sem=pack_arrive.at[place],
                device_id=(place, lon),
                device_id_type=mesh_id,
            ).wait_recv()

    start = lat * own - halo + 2 * width
    offset8 = lax.rem(wide - lat * own + halo + width, width)
    inside = offset8 < span
    own8 = (offset8 >= halo) & (offset8 < halo + own)
    for k in range(depth):
        packed = [pack_recv[c, pl.ds(k, SUB, stride=depth), :] for c in range(3)]

        def place_at(c, slot):
            return pltpu.roll(packed[c], lax.rem(start - slot, width), 1)

        mask = jnp.where(offset8 < halo, place_at(1, 2 * span), place_at(1, 2 * span - own))
        mask = jnp.where(own8, place_at(0, 2 * span - halo), mask)
        fields[6, k] = jnp.where(inside, mask, 0.0)
        for i in range(6):
            fields[i, k] = jnp.where(inside, place_at(i // 2, span * (i % 2)), 0.0)

    def field(index, k):
        return fields[index, k]

    is_top = iota((SUB, width), 0) == SUB - 1

    def closed(index, k):
        value = field(index, k)
        return jnp.where(is_top, 0.0, value) if k == top else value

    def above(index, k):
        return field(index, k + 1) if k < top else from_above(field(index, 0))

    n_prev, ne_prev, nw_prev = (from_below(closed(i, top)) for i in (3, 4, 5))
    for k in range(depth):
        ocean = field(6, k)
        ocean_north = above(6, k)
        e_now, n_now, ne_now, nw_now = field(2, k), closed(3, k), closed(4, k), closed(5, k)
        we = e_now * ocean * east(ocean)
        wn = n_now * ocean * ocean_north
        wne = ne_now * ocean * east(ocean_north)
        wnw = nw_now * ocean * west(ocean_north)
        w_e[k] = we
        w_w[k] = west(we)
        w_n[k] = wn
        w_ne[k] = wne
        w_nw[k] = wnw
        sw, se = west(wne), east(wnw)
        if k < top:
            w_s[k + 1] = wn
            w_sw[k + 1] = sw
            w_se[k + 1] = se
        else:
            w_s[0] = from_below(wn)
            w_sw[0] = from_below(sw)
            w_se[0] = from_below(se)
        open_sum = (
            e_now + west(e_now) + n_now + n_prev + ne_now + west(ne_prev) + nw_now + east(nw_prev)
        )
        diag[k] = ocean * (field(1, k) + open_sum) + (1.0 - ocean)
        n_prev, ne_prev, nw_prev = n_now, ne_now, nw_now
        res_ref[k] = ocean * field(0, k)
        sol_ref[k] = jnp.zeros((SUB, width), jnp.float32)
        dirn[k] = jnp.zeros((SUB, width), jnp.float32)
        along[k] = jnp.zeros((SUB, width), jnp.float32)

    def surface(k):
        ocean = field(6, k)
        return ocean * field(1, k) + (1.0 - ocean)

    low = surface(0) + w_s[0]
    high = surface(top) + w_n[top]
    for k in range(half):
        up, j = k, top - k
        g_low = 1.0 / (low + w_n[up])
        g_high = 1.0 / (high + w_s[j])
        f_g[up] = g_low
        f_g[j] = g_high
        if k < half - 1:
            f_a[up + 1] = w_n[up] * g_low
            f_a[j - 1] = w_s[j] * g_high
            low = surface(up + 1) + w_n[up] * (low * g_low)
            high = surface(j - 1) + w_s[j] * (high * g_high)
    mid = w_n[half - 1]
    inv_det = 1.0 / (low * high + mid * (low + high))
    mid_ll = (high + mid) * inv_det
    mid_lh = mid * inv_det
    mid_hh = (low + mid) * inv_det

    def line(read, write):
        y, z = read(0), read(top)
        ys, zs = [y], [z]
        u_ref[0] = y
        u_ref[top] = z
        for k in range(1, half):
            j = top - k
            y = read(k) + f_a[k] * y
            z = read(j) + f_a[j] * z
            u_ref[k] = y
            u_ref[j] = z
        x = mid_ll * y + mid_lh * z
        v = mid_lh * y + mid_hh * z
        write(half - 1, x)
        write(half, v)
        for k in range(half - 2, -1, -1):
            j = top - k
            x = f_g[k] * u_ref[k] + f_a[k + 1] * x
            v = f_g[j] * u_ref[j] + f_a[j - 1] * v
            write(k, x)
            write(j, v)

    zero = jnp.zeros((SUB, width), jnp.float32)
    line(lambda k: w_s[0] if k == 0 else zero, lambda k, v: resp0.__setitem__(k, v))
    line(lambda k: w_n[top] if k == top else zero, lambda k, v: resp1.__setitem__(k, v))

    a, b, c, d = resp0[0], resp1[0], resp0[top], resp1[top]
    plan = []
    stride = 1
    while stride < SUB:
        def below(x, stride=stride):
            return pltpu.roll(x, stride, 0)

        def over(x, stride=stride):
            return pltpu.roll(x, SUB - stride, 0)

        cb, db = below(c), below(d)
        aa, ba = over(a), over(b)
        m00, m01 = 1.0 - a * db, -b * aa
        m10, m11 = -c * db, 1.0 - d * aa
        inv = 1.0 / (m00 * m11 - m01 * m10)
        i00, i01, i10, i11 = m11 * inv, -m01 * inv, -m10 * inv, m00 * inv
        t0, t1 = i00 * a + i01 * c, i00 * b + i01 * d
        t2, t3 = i10 * a + i11 * c, i10 * b + i11 * d
        plan.append((stride, i00, i01, i10, i11, t0, t1, t2, t3))
        a, b, c, d = t0 * cb, t1 * ba, t2 * cb, t3 * ba
        stride *= 2

    def interface(p, q):
        for stride, i00, i01, i10, i11, t0, t1, t2, t3 in plan:
            qb = pltpu.roll(q, stride, 0)
            pa = pltpu.roll(p, SUB - stride, 0)
            p, q = (
                (i00 * p + i01 * q) + (t0 * qb + t1 * pa),
                (i10 * p + i11 * q) + (t2 * qb + t3 * pa),
            )
        return from_below(q), from_above(p)

    @pl.when(at_top)
    def _():
        def one(step, carry):
            top_copy(step).wait_send()
            return carry

        lax.fori_loop(1, n_dev, one, 0, unroll=n_dev <= 64)

    for b in range(lon_count):

        @pl.when(jnp.logical_or(lat != lat_count - 1, lon != b))
        def _(b=b):
            pltpu.make_async_remote_copy(
                src_ref=top_msg,
                dst_ref=top_recv.at[b],
                send_sem=top_send.at[0],
                recv_sem=top_arrive.at[b],
                device_id=(lat_count - 1, b),
                device_id_type=mesh_id,
            ).wait_recv()

    whole_north = jnp.concatenate([top_recv[b][0:1] for b in range(lon_count)], axis=0)
    whole_ocean = jnp.concatenate([top_recv[b][1:2] for b in range(lon_count)], axis=0)
    total_cols = lon_count * width
    back = total_cols - 1 - shift_ref[0]
    row_shift = back // width
    lane_shift = lax.rem(back, width)
    lanes = iota((lon_count, width), 1)

    def facing(rows):
        flipped = jnp.concatenate(
            [rows[b : b + 1] for b in range(lon_count - 1, -1, -1)], axis=0
        )
        index = width - 1 - lax.rem(lanes + lane_shift, width)
        turned = jnp.take_along_axis(flipped, index, axis=1)
        first = pltpu.roll(turned, lax.rem(lon_count - row_shift, lon_count), 0)
        second = pltpu.roll(turned, lon_count - 1 - row_shift, 0)
        return jnp.where(lanes + lane_shift < width, first, second)

    fold_open = 0.5 * (whole_north + facing(whole_north))
    fold_ref[0] = fold_open * whole_ocean
    fold_ref[1] = fold_open * whole_ocean * facing(whole_ocean)
    rows_id = iota((lon_count, width), 0)
    reach = lax.rem(lanes - lat * own + width + (width - own) // 2, width) - (width - own) // 2
    spill = lat * own + reach
    home = jnp.where(spill < 0, -1, jnp.where(spill >= width, 1, 0))
    pick = rows_id == lax.rem(lon + home + lon_count, lon_count)

    def iterate(step, carry):
        rz_old, step_old = carry
        parity = lax.rem(step, 2)
        line(lambda k: res_ref[k], lambda k, v: u_ref.__setitem__(k, v))
        below, over = interface(u_ref[0], u_ref[top])
        accs = [zero, zero, zero, zero]

        def finish(k):
            value = u_ref[k] + below * resp0[k] + over * resp1[k]
            u_ref[k] = value
            accs[k % 2] = accs[k % 2] + res_ref[k] * value
            return (value, east(value), west(value))

        last = finish(top)
        first = finish(0)
        prev = tuple(from_below(x) for x in last)
        now = first
        for k in range(depth):
            if k < top - 1:
                nxt = finish(k + 1)
            elif k == top - 1:
                nxt = last
            else:
                nxt = tuple(from_above(x) for x in first)
            value = (
                (diag[k] * now[0] - w_e[k] * now[1] - w_w[k] * now[2])
                - (w_n[k] * nxt[0] + w_ne[k] * nxt[1] + w_nw[k] * nxt[2])
                - (w_s[k] * prev[0] + w_se[k] * prev[1] + w_sw[k] * prev[2])
            )
            img[k] = value
            accs[2 + k % 2] = accs[2 + k % 2] + now[0] * value
            prev, now = now, nxt
        rz_part = jnp.sum(jnp.where(own_row, accs[0] + accs[1], 0.0), keepdims=True)
        curve_part = jnp.sum(jnp.where(own_row, accs[2] + accs[3], 0.0), keepdims=True)
        row = jnp.where(own_row, last[0][SUB - 1 :], 0.0)
        row = jnp.where(relative == own, rz_part, row)
        row = jnp.where(relative == own + 1, curve_part, row)
        send_all(parity, row)
        top_row, rest = wait_all(parity)
        rest_lane = lax.rem(lanes, own)
        fold_image = fold_ref[0] * top_row - fold_ref[1] * facing(top_row)
        rz = jnp.sum(jnp.where(rest_lane == 0, rest, 0.0), keepdims=True)
        curve = jnp.sum(
            jnp.where(rest_lane == 1, rest, 0.0) + fold_image * top_row, keepdims=True
        )
        fix = jnp.sum(jnp.where(pick, fold_image, 0.0), axis=0, keepdims=True)
        img[top] = img[top] + jnp.where(is_top, fix, 0.0)
        ratio = jnp.where(step == 0, 0.0, rz / rz_old)
        length = rz / (curve - ratio * rz / step_old)
        ratio_v = jnp.broadcast_to(ratio, (SUB, width))
        length_v = jnp.broadcast_to(length, (SUB, width))
        for k in range(depth):
            toward = u_ref[k] + ratio_v * dirn[k]
            moved = img[k] + ratio_v * along[k]
            dirn[k] = toward
            along[k] = moved
            sol_ref[k] = sol_ref[k] + length_v * toward
            res_ref[k] = res_ref[k] - length_v * moved
        return (rz, length)

    one = jnp.ones((1, 1), jnp.float32)
    lax.fori_loop(0, ITERS, iterate, (one, one))

    quarter = depth // 2
    place8 = lax.rem(wide - lat * own + width, width)
    for k in range(quarter):
        row = jnp.where(place8 < own, sol_ref[k], pltpu.roll(res_ref[k], own, 1))
        later = jnp.where(
            place8 < 3 * own,
            pltpu.roll(sol_ref[k + quarter], 2 * own, 1),
            pltpu.roll(res_ref[k + quarter], 3 * own, 1),
        )
        back_msg[pl.ds(k, SUB, stride=quarter), :] = jnp.where(place8 < 2 * own, row, later)
    part = rows // 2

    def back_copy(place):
        return pltpu.make_async_remote_copy(
            src_ref=back_msg.at[place * part : (place + 1) * part],
            dst_ref=back_recv.at[lat],
            send_sem=back_send.at[place],
            recv_sem=back_arrive.at[lat],
            device_id=(place, lon),
            device_id_type=mesh_id,
        )

    for place in range(lat_count):

        @pl.when(lat != place)
        def _(place=place):
            back_copy(place).start()

    back_recv[lat] = back_msg[pl.ds(pl.multiple_of(lat * part, part), part), :]
    for place in range(lat_count):

        @pl.when(lat != place)
        def _(place=place):
            back_copy(place).wait_send()
            pltpu.make_async_remote_copy(
                src_ref=back_msg.at[place * part : (place + 1) * part],
                dst_ref=back_recv.at[place],
                send_sem=back_send.at[place],
                recv_sem=back_arrive.at[place],
                device_id=(place, lon),
                device_id_type=mesh_id,
            ).wait_recv()

    for v in range(part // SUB):
        block, k = divmod(v * SUB, quarter)
        parts = [jnp.zeros((SUB, width), jnp.float32)] * 4
        for place in range(lat_count):
            piece = back_recv[place, v * SUB : (v + 1) * SUB]
            mine = (wide >= place * own) & (wide < (place + 1) * own)
            for i in range(4):
                moved = pltpu.roll(piece, (width - i * own) % width, 1) if i else piece
                parts[i] = jnp.where(mine, moved, parts[i])
        low = block * depth + k
        sol_out[low : low + SUB] = parts[0]
        res_out[low : low + SUB] = parts[1]
        sol_out[low + quarter : low + quarter + SUB] = parts[2]
        res_out[low + quarter : low + quarter + SUB] = parts[3]


def shards(
    right_side,
    surface_term,
    east_coupling,
    north_coupling,
    neast_coupling,
    nwest_coupling,
    land_sea,
    fold_map,
):
    rows, width = right_side.shape
    lat_count = lax.axis_size("lat")
    lon_count = lax.axis_size("lon")
    lon = lax.axis_index("lon")
    n_dev = lat_count * lon_count
    depth = rows * lat_count // SUB
    columns = lon_count * width
    turn = lax.rem(fold_map[:1] + lon * width, columns)

    block = pltpu.VMEM((depth, SUB, width), jnp.float32)
    answer = jax.ShapeDtypeStruct((rows, width), jnp.float32)
    vmem = pl.BlockSpec(memory_space=pltpu.VMEM)
    dma = pltpu.SemaphoreType.DMA

    def held(*shape):
        return pltpu.VMEM((*shape, width), jnp.float32)

    return pl.pallas_call(
        functools.partial(kernel, lat_count, lon_count),
        out_shape=(answer, answer),
        in_specs=[pl.BlockSpec(memory_space=pltpu.SMEM)] + [vmem] * 7,
        out_specs=(vmem, vmem),
        scratch_shapes=[block] * 19
        + [
            held(7, depth, SUB),
            held(2, 1),
            held(2, n_dev, 1),
            held(2, lon_count),
            held(2),
            held(lon_count, 2),
            held(2, rows),
            held(2, rows),
            held(lat_count, 3, rows),
            held(3, lat_count * rows),
            held(lat_count * rows // 2),
            held(lat_count, rows // 2),
            dma((2, n_dev)),
            dma((2, n_dev)),
            dma((n_dev,)),
            dma((lon_count,)),
            dma((2,)),
            dma((2,)),
            dma((lat_count,)),
            dma((lat_count,)),
            dma((lat_count,)),
            dma((lat_count,)),
        ],
        compiler_params=pltpu.CompilerParams(collective_id=0, has_side_effects=True),
    )(
        turn,
        right_side,
        surface_term,
        east_coupling,
        north_coupling,
        neast_coupling,
        nwest_coupling,
        land_sea,
    )


def solution(mesh):
    return jax.shard_map(
        shards,
        mesh=mesh,
        in_specs=(P("lat", "lon"),) * 7 + (P("lon"),),
        out_specs=(P("lat", "lon"), P("lat", "lon")),
        check_vma=False,
    )
```

profile of v0, /device:TPU:0, one launch (start us, length us, event | category | flops | bytes accessed | tf_op | source)
XLA Modules:
  0.0 79.1 jit_solution(5038772338259215984)
XLA Ops:
  0.6 0.0 copy-start.1
  0.6 0.6 copy-done.1
  1.3 75.6 %shard_map.95 = (f32[128,128]{1,0:T(8,128)}, f32[128,128]{1,0:T(8,128)}) custom-call(s32[1]{0:T(128)S(6)} %rem.18.shift_ref, f32[128,128]{1,0:T(8,128)} %right_ref.1, f32[128,128]{1,0:T(8,128)} %surface_ref.1, f32[128,128]{1,0:T(8,128)} %east_ref.1, f32[128,128]{1,0:T(8,128)} %north_ref.1, f32[128,128]{1,0:T(8,128)} %neast_ref.1, f32[128,128]{1,0:T(8,128)} %nwest_ref.1, ...), custom_call_target="tpu_custom_call" | custom-call | tf_op jit(solution)/shard_map/pallas_call | solution.py:621
  77.0 0.0 copy-start
  77.0 1.5 %copy.12 = f32[128,128]{1,0:T(8,128)} copy(f32[128,128]{1,0:T(8,128)} %get-tuple-element.4) | data formatting | bytes 131072
  78.5 0.0 copy-done
  78.5 0.6 copy.13
Async XLA Ops:
  0.6 0.7 copy-start.1
  77.0 1.5 %copy-start = (f32[128,128]{1,0:T(8,128)S(1)}, f32[128,128]{1,0:T(8,128)}, u32[]{:S(2)}) copy-start(f32[128,128]{1,0:T(8,128)} %get-tuple-element.5) | copy-start | bytes 196612
where the time goes:
time: 79.4 us; the launch traced here: 79.1 us
  Pallas kernels  75.6 us (95%)
  local copies, waits for them, and re-layouts  2.79 us (4%)
    pallas_call x1, Pallas kernels, shards(): pl.pallas_call(functools.partial(kernel, lat_count, lon_count), out_shape...  75.6 us
    unnamed x6, local copies, waits for them, and re-layouts  2.79 us

commit v1 on v0

--- a/solution.py
+++ b/solution.py
@@ -57,7 +57,7 @@
     f_g,
     resp0,
     resp1,
-    u_ref,
+    u_pair,
     img,
     dirn,
     along,
@@ -113,33 +113,51 @@
     relative = lax.rem(lane - lat * own + width, width)
     own_row = relative < own
 
-    def copy_to(parity, step):
-        peer = lax.rem(me + step, n_dev)
+    def alternate(size):
+        ring = []
+        for i in range(1, size // 2 + 1):
+            ring += [size - i, i]
+        return list(dict.fromkeys([*ring, 0]))
+
+    lats = {d: lax.rem(lat + d, lat_count) for d in range(lat_count)}
+    lons = {d: lax.rem(lon + d, lon_count) for d in range(lon_count)}
+    peers = [(p, q) for q in alternate(lon_count) for p in alternate(lat_count) if p or q]
+
+    def copy_to(parity, place):
         return pltpu.make_async_remote_copy(
             src_ref=msg.at[parity],
             dst_ref=recv.at[parity, me],
-            send_sem=send_sem.at[parity, step],
-            recv_sem=recv_sem.at[parity, step],
-            device_id=(peer // lon_count, lax.rem(peer, lon_count)),
+            send_sem=send_sem.at[parity],
+            recv_sem=recv_sem.at[parity],
+            device_id=place,
             device_id_type=pl.DeviceIdType.MESH,
         )
 
     def send_all(parity, row):
         msg[parity] = row
         recv[parity, me] = row
+        if n_dev <= 64:
+            for p, q in peers:
+                copy_to(parity, (lats[p], lons[q])).start()
+            return
 
         def one(step, carry):
-            copy_to(parity, step).start()
+            peer = lax.rem(me + step, n_dev)
+            copy_to(parity, (peer // lon_count, lax.rem(peer, lon_count))).start()
             return carry
 
-        lax.fori_loop(1, n_dev, one, 0, unroll=n_dev <= 64)
+        lax.fori_loop(1, n_dev, one, 0)
 
     def wait_all(parity):
-        def one(step, carry):
-            copy_to(parity, step).wait()
-            return carry
-
-        lax.fori_loop(1, n_dev, one, 0, unroll=n_dev <= 64)
+        every = recv.at[parity, 0 : n_dev - 1]
+        pltpu.make_async_remote_copy(
+            src_ref=every,
+            dst_ref=every,
+            send_sem=send_sem.at[parity],
+            recv_sem=recv_sem.at[parity],
+            device_id=(lats[0], lons[1]),
+            device_id_type=pl.DeviceIdType.MESH,
+        ).wait()
         top_row = jnp.zeros((lon_count, width), jnp.float32)
         rest = jnp.zeros((lon_count, width), jnp.float32)
         for place in range(lat_count):
@@ -363,7 +381,7 @@
     mid_lh = mid * inv_det
     mid_hh = (low + mid) * inv_det
 
-    def line(read, write):
+    def line(read, write, u_ref=u_pair.at[0]):
         y, z = read(0), read(top)
         ys, zs = [y], [z]
         u_ref[0] = y
@@ -470,9 +488,10 @@
     pick = rows_id == lax.rem(lon + home + lon_count, lon_count)
 
     def iterate(step, carry):
-        rz_old, step_old = carry
+        rz_old, step_old, ratio_old = carry
         parity = lax.rem(step, 2)
-        line(lambda k: res_ref[k], lambda k, v: u_ref.__setitem__(k, v))
+        u_ref = u_pair.at[parity]
+        line(lambda k: res_ref[k], lambda k, v: u_ref.__setitem__(k, v), u_ref)
         below, over = interface(u_ref[0], u_ref[top])
         accs = [zero, zero, zero, zero]
 
@@ -507,6 +526,7 @@
         row = jnp.where(relative == own, rz_part, row)
         row = jnp.where(relative == own + 1, curve_part, row)
         send_all(parity, row)
+        advance(1 - parity, ratio_old, jnp.where(step == 0, 0.0, step_old))
         top_row, rest = wait_all(parity)
         rest_lane = lax.rem(lanes, own)
         fold_image = fold_ref[0] * top_row - fold_ref[1] * facing(top_row)
@@ -521,16 +541,23 @@
         ratio_v = jnp.broadcast_to(ratio, (SUB, width))
         length_v = jnp.broadcast_to(length, (SUB, width))
         for k in range(depth):
-            toward = u_ref[k] + ratio_v * dirn[k]
             moved = img[k] + ratio_v * along[k]
+            along[k] = moved
+            res_ref[k] = res_ref[k] - length_v * moved
+        return (rz, length, ratio)
+
+    def advance(side, ratio, length):
+        ratio_v = jnp.broadcast_to(ratio, (SUB, width))
+        length_v = jnp.broadcast_to(length, (SUB, width))
+        for k in range(depth):
+            toward = u_pair[side, k] + ratio_v * dirn[k]
             dirn[k] = toward
-            along[k] = moved
             sol_ref[k] = sol_ref[k] + length_v * toward
-            res_ref[k] = res_ref[k] - length_v * moved
-        return (rz, length)
 
     one = jnp.ones((1, 1), jnp.float32)
-    lax.fori_loop(0, ITERS, iterate, (one, one))
+    u_pair[1] = jnp.zeros((depth, SUB, width), jnp.float32)
+    _, length, ratio = lax.fori_loop(0, ITERS, iterate, (one, one, jnp.zeros((1, 1), jnp.float32)))
+    advance((ITERS - 1) % 2, ratio, length)
 
     quarter = depth // 2
     place8 = lax.rem(wide - lat * own + width, width)
@@ -623,7 +650,9 @@
         out_shape=(answer, answer),
         in_specs=[pl.BlockSpec(memory_space=pltpu.SMEM)] + [vmem] * 7,
         out_specs=(vmem, vmem),
-        scratch_shapes=[block] * 19
+        scratch_shapes=[block] * 13
+        + [held(2, depth, SUB)]
+        + [block] * 5
         + [
             held(7, depth, SUB),
             held(2, 1),
@@ -637,8 +666,8 @@
             held(3, lat_count * rows),
             held(lat_count * rows // 2),
             held(lat_count, rows // 2),
-            dma((2, n_dev)),
-            dma((2, n_dev)),
+            dma((2,)),
+            dma((2,)),
             dma((n_dev,)),
             dma((lon_count,)),
             dma((2,)),

time: 79.4 us -> 77.4 us (0.975)
  Pallas kernels: 75.6 us -> 73.6 us
    pallas_call x1, Pallas kernels: 75.6 us -> 73.6 us  [shards(): pl.pallas_call(functools.partial(kernel, lat_count, lon_count), out_shape...]
where the time goes in v1:
time: 77.4 us; the launch traced here: 77.1 us
  Pallas kernels  73.6 us (95%)
  local copies, waits for them, and re-layouts  2.79 us (4%)
    pallas_call x1, Pallas kernels, shards(): pl.pallas_call(functools.partial(kernel, lat_count, lon_count), out_shape...  73.6 us
    unnamed x6, local copies, waits for them, and re-layouts  2.79 us

profile of v1, /device:TPU:0, one launch (start us, length us, event | category | flops | bytes accessed | tf_op | source)
XLA Modules:
  0.0 77.1 jit_solution(10100376775345235612)
XLA Ops:
  0.6 0.0 copy-start.1
  0.6 0.6 copy-done.1
  1.3 73.6 %shard_map.95 = (f32[128,128]{1,0:T(8,128)}, f32[128,128]{1,0:T(8,128)}) custom-call(s32[1]{0:T(128)S(6)} %rem.18.shift_ref, f32[128,128]{1,0:T(8,128)} %right_ref.1, f32[128,128]{1,0:T(8,128)} %surface_ref.1, f32[128,128]{1,0:T(8,128)} %east_ref.1, f32[128,128]{1,0:T(8,128)} %north_ref.1, f32[128,128]{1,0:T(8,128)} %neast_ref.1, f32[128,128]{1,0:T(8,128)} %nwest_ref.1, ...), custom_call_target="tpu_custom_call" | custom-call | tf_op jit(solution)/shard_map/pallas_call | solution.py:648
  75.0 0.0 copy-start
  75.0 1.5 %copy.12 = f32[128,128]{1,0:T(8,128)} copy(f32[128,128]{1,0:T(8,128)} %get-tuple-element.4) | data formatting | bytes 131072
  76.5 0.0 copy-done
  76.5 0.6 copy.13
Async XLA Ops:
  0.6 0.7 copy-start.1
  75.0 1.5 %copy-start = (f32[128,128]{1,0:T(8,128)S(1)}, f32[128,128]{1,0:T(8,128)}, u32[]{:S(2)}) copy-start(f32[128,128]{1,0:T(8,128)} %get-tuple-element.5) | copy-start | bytes 196612
